TPU v7x, 32 devices: a whole 2x2x4 slice. The times are simulated.
32 devices in a mesh: dp: 4 (over z), row: 2 (over x), col: 4 (over y, core).
Axes of the slice: x: 2, y: 2, z: 4, core: 2. Of those that a mesh axis runs over, the one named last changes fastest.
Arguments:
- grad: bfloat16 [4, 4096, 14336], P('dp', 'row', 'col'), may hold values from -6 to 6
- error: bfloat16 [4, 4096, 14336], P('dp', 'row', 'col'), may hold values from -6 to 6
- q_init: float32 [14336, 128], P('col'), may hold values from -6 to 6
Outputs:
- new_error: bfloat16 [4, 4096, 14336], P('dp', 'row', 'col')
- q_factor: float32 [14336, 128], P('col')
All inputs are finite; a program needn't handle non-finite values.
Results may differ from a plain program's by a relative error of at most 0.001.
Values sent between devices are 32-bit elements; how exact they have to be, the bound alone decides.
A program may use at most 128 MiB of HBM per device.

v0:
```python
import jax
import jax.numpy as jnp
from jax import lax
from jax.sharding import PartitionSpec as P

ITERS = 2


def solve_rows(p_mat, gram):
    lower = jnp.linalg.cholesky(gram)
    return jax.scipy.linalg.solve_triangular(lower, p_mat.T, lower=True).T


def self_gram(p_mat):
    return jnp.dot(
        p_mat.T, p_mat, precision=lax.Precision.HIGHEST, preferred_element_type=jnp.float32
    )


def shards(grad, error, q_init):
    comp = grad[0].astype(jnp.float32) + error[0].astype(jnp.float32)
    scale = 1.0 / lax.axis_size("dp")
    q_mat = q_init
    p_hat = None
    for step in range(ITERS):
        partial_value = jnp.dot(
            comp, q_mat, precision=lax.Precision.HIGHEST, preferred_element_type=jnp.float32
        )
        summed = lax.psum(lax.psum(partial_value, "col"), "dp")
        p_mat = summed * scale
        gram = lax.psum(self_gram(p_mat), "row")
        p_hat = solve_rows(p_mat, gram)
        term = lax.dot_general(
            comp,
            p_hat,
            (((0,), (0,)), ((), ())),
            precision=lax.Precision.HIGHEST,
            preferred_element_type=jnp.float32,
        )
        q_mat = lax.psum(term, ("dp", "row")) * scale
    approx = jnp.dot(
        p_hat, q_mat.T, precision=lax.Precision.HIGHEST, preferred_element_type=jnp.float32
    )
    new_error = (comp - approx).astype(jnp.bfloat16)[None]
    return (new_error, q_mat)


def solution(mesh):
    in_specs = (P("dp", "row", "col"), P("dp", "row", "col"), P("col", None))
    out_specs = (P("dp", "row", "col"), P("col", None))
    return jax.shard_map(shards, mesh=mesh, in_specs=in_specs, out_specs=out_specs, check_vma=False)
```

profile of v0, /device:TPU:0, one launch (start us, length us, event | category | flops | bytes accessed | tf_op | source)
XLA Modules:
  0.0 686.6 jit_solution(13986567056478800305)
XLA Ops:
  7.2 0.0 copy-start
  7.2 0.0 all-reduce.9.cloned.1.call-start
  7.2 1.4 copy-done
  8.7 28.2 %fusion.6 = f32[2048,128]{1,0:T(8,128)} fusion(f32[3584,128]{1,0:T(8,128)S(1)} %copy-done, bf16[1,2048,3584]{2,1,0:T(8,128)(2,1)} %param.7, bf16[1,2048,3584]{2,1,0:T(8,128)(2,1)} %param.6), kind=kOutput, calls=%fused_computation.7 | convolution fusion | flops 11296309248 | bytes 32243712 | tf_op jit(solution)/shard_map/dot_general | solution.py:26
  36.9 0.0 all-reduce.9.cloned.1.call-update
  36.9 0.0 all-reduce.11.cloned.1.call-start
  37.0 39.1 %all-reduce.9.cloned.1.call-done = f32[2048,128]{1,0:T(8,128)} async-done(((f32[2048,128]{1,0:T(8,128)}), f32[2048,128]{1,0:T(8,128)}) %all-reduce.9.cloned.1.call-update) | async-done | bytes 1048592 | tf_op jit(solution)/shard_map/psum | solution.py:29
  76.1 0.0 all-reduce.11.cloned.1.call-update
  76.1 0.0 all-reduce.13.cloned.1.call-start
  76.2 54.7 %all-reduce.11.cloned.1.call-done = f32[2048,128]{1,0:T(8,128)} async-done(((f32[2048,128]{1,0:T(8,128)}), f32[2048,128]{1,0:T(8,128)}) %all-reduce.11.cloned.1.call-update) | async-done | bytes 1048592 | tf_op jit(solution)/shard_map/psum | solution.py:29
  130.9 4.0 fusion.19
  134.9 0.0 all-reduce.13.cloned.1.call-update
  134.9 0.2 all-reduce.15.cloned.1.call-start
  135.1 20.1 %all-reduce.13.cloned.1.call-done = f32[128,128]{0,1:T(8,128)} async-done(((f32[128,128]{0,1:T(8,128)}), f32[128,128]{0,1:T(8,128)}) %all-reduce.13.cloned.1.call-update) | async-done | bytes 65552 | tf_op jit(solution)/shard_map/psum | solution.py:31
  155.3 0.9 copy.6
  156.2 0.9 fusion.31
  157.1 11.7 %cholesky.44 = f32[128,128]{1,0:T(8,128)S(1)} custom-call(f32[128,128]{1,0:T(8,128)S(1)} %fusion.31), custom_call_target="Cholesky" | custom-call | tf_op jit(solution)/shard_map/jit(cholesky)/cholesky | solution.py:10
  168.8 0.6 compare_reduce_fusion.1
  169.4 0.7 fusion.26
  170.1 9.8 %custom-call.6 = f32[1,128,128]{1,2,0:T(8,128)S(1)} custom-call(f32[1,128,128]{2,1,0:T(8,128)S(1)} %fusion.26), custom_call_target="InvertDiagBlocksLowerTriangular" | custom-call | tf_op jit(solution)/shard_map/jit(_solve_triangular)/triangular_solve | solution.py:11
  179.9 2.3 fusion.13
  182.2 50.6 %fusion.4 = f32[3584,128]{1,0:T(8,128)} fusion(f32[128,2048]{1,0:T(8,128)S(1)} %fusion.13, bf16[1,2048,3584]{2,1,0:T(8,128)(2,1)} %param.7, bf16[1,2048,3584]{2,1,0:T(8,128)(2,1)} %param.6), kind=kOutput, calls=%fused_computation.5 | convolution fusion | flops 11296309248 | bytes 32243712 | tf_op jit(solution)/shard_map/dot_general | solution.py:33
  232.8 0.0 all-reduce.15.cloned.1.call-update
  232.9 0.0 all-reduce.17.cloned.1.call-start
  232.9 95.9 %all-reduce.15.cloned.1.call-done = f32[3584,128]{1,0:T(8,128)} async-done(((f32[3584,128]{1,0:T(8,128)}), f32[3584,128]{1,0:T(8,128)}) %all-reduce.15.cloned.1.call-update) | async-done | bytes 1835024 | tf_op jit(solution)/shard_map/psum | solution.py:40
  328.8 28.4 %fusion.2 = f32[2048,128]{1,0:T(8,128)} fusion(bf16[1,2048,3584]{2,1,0:T(8,128)(2,1)} %param.7, bf16[1,2048,3584]{2,1,0:T(8,128)(2,1)} %param.6, f32[3584,128]{1,0:T(8,128)} %all-reduce.15.cloned.1.call-done), kind=kOutput, calls=%fused_computation.3 | convolution fusion | flops 11296768000 | bytes 32243712 | tf_op jit(solution)/shard_map/dot_general | solution.py:26
  357.3 0.0 all-reduce.17.cloned.1.call-update
  357.3 0.0 all-reduce.19.cloned.1.call-start
  357.3 35.9 %all-reduce.17.cloned.1.call-done = f32[2048,128]{1,0:T(8,128)} async-done(((f32[2048,128]{1,0:T(8,128)}), f32[2048,128]{1,0:T(8,128)}) %all-reduce.17.cloned.1.call-update) | async-done | bytes 1048592 | tf_op jit(solution)/shard_map/psum | solution.py:29
  393.3 0.0 all-reduce.19.cloned.1.call-update
  393.3 0.0 all-reduce.21.cloned.1.call-start
  393.3 54.5 %all-reduce.19.cloned.1.call-done = f32[2048,128]{1,0:T(8,128)} async-done(((f32[2048,128]{1,0:T(8,128)}), f32[2048,128]{1,0:T(8,128)}) %all-reduce.19.cloned.1.call-update) | async-done | bytes 1048592 | tf_op jit(solution)/shard_map/psum | solution.py:29
  447.9 4.0 fusion.16
  451.9 0.0 all-reduce.21.cloned.1.call-update
  451.9 0.5 all-reduce.23.cloned.1.call-start
  452.4 19.9 %all-reduce.21.cloned.1.call-done = f32[128,128]{0,1:T(8,128)} async-done(((f32[128,128]{0,1:T(8,128)}), f32[128,128]{0,1:T(8,128)}) %all-reduce.21.cloned.1.call-update) | async-done | bytes 65552 | tf_op jit(solution)/shard_map/psum | solution.py:31
  472.3 0.9 copy.8
  473.2 0.9 fusion.29
  474.1 11.7 %cholesky.55 = f32[128,128]{1,0:T(8,128)S(1)} custom-call(f32[128,128]{1,0:T(8,128)S(1)} %fusion.29), custom_call_target="Cholesky" | custom-call | tf_op jit(solution)/shard_map/jit(cholesky)/cholesky | solution.py:10
  485.8 0.6 compare_reduce_fusion
  486.4 0.7 fusion.27
  487.1 9.8 %custom-call.7 = f32[1,128,128]{1,2,0:T(8,128)S(1)} custom-call(f32[1,128,128]{2,1,0:T(8,128)S(1)} %fusion.27), custom_call_target="InvertDiagBlocksLowerTriangular" | custom-call | tf_op jit(solution)/shard_map/jit(_solve_triangular)/triangular_solve | solution.py:11
  496.9 2.3 fusion.11
  499.2 50.5 %fusion = f32[3584,128]{1,0:T(8,128)} fusion(f32[128,2048]{1,0:T(8,128)S(1)} %fusion.11, bf16[1,2048,3584]{2,1,0:T(8,128)(2,1)} %param.7, bf16[1,2048,3584]{2,1,0:T(8,128)(2,1)} %param.6), kind=kOutput, calls=%fused_computation.1 | convolution fusion | flops 11296309248 | bytes 32243712 | tf_op jit(solution)/shard_map/dot_general | solution.py:33
  549.7 0.0 all-reduce.23.cloned.1.call-update
  549.7 96.0 %all-reduce.23.cloned.1.call-done = f32[3584,128]{1,0:T(8,128)} async-done(((f32[3584,128]{1,0:T(8,128)}), f32[3584,128]{1,0:T(8,128)}) %all-reduce.23.cloned.1.call-update) | async-done | bytes 1835024 | tf_op jit(solution)/shard_map/psum | solution.py:40
  645.7 1.6 broadcast_multiply_fusion
  647.3 32.2 %fusion.9 = bf16[1,2048,3584]{2,1,0:T(8,128)(2,1)} fusion(f32[128,2048]{1,0:T(8,128)S(1)} %fusion.11, f32[3584,128]{1,0:T(8,128)S(1)} %broadcast_multiply_fusion, bf16[1,2048,3584]{2,1,0:T(8,128)(2,1)} %param.7, bf16[1,2048,3584]{2,1,0:T(8,128)(2,1)} %param.6), kind=kOutput, calls=%fused_computation.11 | convolution fusion | flops 11310989312 | bytes 46923776 | tf_op jit(solution)/shard_map/dot_general | solution.py:41
  (4 shorter events, 0.1 us)
Async XLA Ops:
  7.2 1.5 copy-start
  7.2 68.9 %all-reduce.9.cloned.1.call-start = ((), (), s32[]{:S(2)}) async-start(), calls=%async_computation | async-start | bytes 2097152 | tf_op jit(solution)/shard_map/psum | solution.py:29
  36.9 93.9 %all-reduce.11.cloned.1.call-start = ((), (), s32[]{:S(2)}) async-start(), calls=%async_computation.1 | async-start | bytes 2097152 | tf_op jit(solution)/shard_map/psum | solution.py:29
  76.1 79.1 %all-reduce.13.cloned.1.call-start = ((), (), s32[]{:S(2)}) async-start(), calls=%async_computation.2 | async-start | bytes 131072 | tf_op jit(solution)/shard_map/psum | solution.py:31
  134.9 193.9 %all-reduce.15.cloned.1.call-start = ((), (), s32[]{:S(2)}) async-start(), calls=%async_computation.3 | async-start | bytes 3670016 | tf_op jit(solution)/shard_map/psum | solution.py:40
  232.9 160.4 %all-reduce.17.cloned.1.call-start = ((), (), s32[]{:S(2)}) async-start(), calls=%async_computation.4 | async-start | bytes 2097152 | tf_op jit(solution)/shard_map/psum | solution.py:29
  357.3 90.6 %all-reduce.19.cloned.1.call-start = ((), (), s32[]{:S(2)}) async-start(), calls=%async_computation.5 | async-start | bytes 2097152 | tf_op jit(solution)/shard_map/psum | solution.py:29
  393.3 79.0 %all-reduce.21.cloned.1.call-start = ((), (), s32[]{:S(2)}) async-start(), calls=%async_computation.6 | async-start | bytes 131072 | tf_op jit(solution)/shard_map/psum | solution.py:31
  451.9 193.8 %all-reduce.23.cloned.1.call-start = ((), (), s32[]{:S(2)}) async-start(), calls=%async_computation.7 | async-start | bytes 3670016 | tf_op jit(solution)/shard_map/psum | solution.py:40
  647.3 32.2 %copy-start.1 = (f32[3584,128]{1,0:T(8,128)}, f32[3584,128]{1,0:T(8,128)S(1)}, u32[]{:S(2)}) copy-start(f32[3584,128]{1,0:T(8,128)S(1)} %broadcast_multiply_fusion) | copy-start | bytes 5505028
Sparse Core Ops, SparseCore 0:
  37.1 39.0 all-reduce.8
  78.5 52.3 all-reduce.10
  135.0 20.1 all-reduce.12
  233.0 95.8 all-reduce.14
  357.4 35.8 all-reduce.16
  395.5 52.3 all-reduce.18
  452.0 20.1 all-reduce.20
  549.8 95.8 all-reduce.22
where the time goes:
time: 693 us; the launch traced here: 687 us
  waiting for transfers between devices  416 us (60%)
  matrix products  203 us (29%)
  other arithmetic  49 us (7%)
  between operations  14.5 us (2%)
    psum x2, waiting for transfers between devices, shards(): q_mat = lax.psum(term, ('dp', 'row')) * scale  192 us
    psum x4, waiting for transfers between devices, shards(): summed = lax.psum(lax.psum(partial_value, 'col'), 'dp')  184 us
    dot_general x2, matrix products, shards(): lax.dot_general(comp, p_hat, (((0,), (0,)), ((), ())), precision=lax.Prec...  101 us
    dot_general x2, matrix products, shards(): jnp.dot(comp, q_mat, precision=lax.Precision.HIGHEST, preferred_element_t...  56.7 us
    psum x2, waiting for transfers between devices, shards(): gram = lax.psum(self_gram(p_mat), 'row')  40 us
    dot_general x1, matrix products, shards(): jnp.dot(p_hat, q_mat.T, precision=lax.Precision.HIGHEST, preferred_elemen...  32.2 us
    another operation x6, other arithmetic, solve_rows(): lower = jnp.linalg.cholesky(gram)  24.8 us
    another operation x4, other arithmetic, solve_rows(): return jax.scipy.linalg.solve_triangular(lower, p_mat.T, lower=True).T  20.9 us
  transfers between devices with their start and end apart: 8, of which 8 were waited for; matrix products, arithmetic and copies ran while one was open for 0% of the time, Pallas kernels for 0%

commit v1 on v0

--- a/solution.py
+++ b/solution.py
@@ -37,7 +37,7 @@
             precision=lax.Precision.HIGHEST,
             preferred_element_type=jnp.float32,
         )
-        q_mat = lax.psum(term, ("dp", "row")) * scale
+        q_mat = lax.psum(lax.psum(term, "row"), "dp") * scale
     approx = jnp.dot(
         p_hat, q_mat.T, precision=lax.Precision.HIGHEST, preferred_element_type=jnp.float32
     )

time: 693 us -> 775 us (1.12)
  waiting for transfers between devices: 416 us -> 498 us
    psum x2 -> x4, waiting for transfers between devices: 192 us -> 274 us  [shards(): q_mat = lax.psum(lax.psum(term, 'row'), 'dp') * scale]
  transfers between devices with their start and end apart: 8 -> 10, of which waited for: 8 -> 10; matrix products, arithmetic and copies ran while one was open for 0% -> 0% of each run, Pallas kernels for 0% -> 0%
where the time goes in v1:
time: 775 us; the launch traced here: 769 us
  waiting for transfers between devices  498 us (64%)
  matrix products  202 us (26%)
  other arithmetic  49.2 us (6%)
  between operations  14.5 us (2%)
    psum x4, waiting for transfers between devices, shards(): q_mat = lax.psum(lax.psum(term, 'row'), 'dp') * scale  274 us
    psum x4, waiting for transfers between devices, shards(): summed = lax.psum(lax.psum(partial_value, 'col'), 'dp')  184 us
    dot_general x2, matrix products, shards(): lax.dot_general(comp, p_hat, (((0,), (0,)), ((), ())), precision=lax.Prec...  101 us
    dot_general x2, matrix products, shards(): jnp.dot(comp, q_mat, precision=lax.Precision.HIGHEST, preferred_element_t...  56.5 us
    psum x2, waiting for transfers between devices, shards(): gram = lax.psum(self_gram(p_mat), 'row')  40 us
    dot_general x1, matrix products, shards(): jnp.dot(p_hat, q_mat.T, precision=lax.Precision.HIGHEST, preferred_elemen...  32.2 us
    another operation x6, other arithmetic, solve_rows(): lower = jnp.linalg.cholesky(gram)  24.8 us
    another operation x4, other arithmetic, solve_rows(): return jax.scipy.linalg.solve_triangular(lower, p_mat.T, lower=True).T  20.9 us
  transfers between devices with their start and end apart: 10, of which 10 were waited for; matrix products, arithmetic and copies ran while one was open for 0% of the time, Pallas kernels for 0%

profile of v1, /device:TPU:0, one launch (start us, length us, event | category | flops | bytes accessed | tf_op | source)
XLA Modules:
  0.0 768.7 jit_solution(3016612454252369282)
XLA Ops:
  7.2 0.0 all-reduce.11.cloned.1.call-start
  7.2 1.4 copy-done
  8.7 28.2 %fusion.6 = f32[2048,128]{1,0:T(8,128)} fusion(f32[3584,128]{1,0:T(8,128)S(1)} %copy-done, bf16[1,2048,3584]{2,1,0:T(8,128)(2,1)} %param.7, bf16[1,2048,3584]{2,1,0:T(8,128)(2,1)} %param.6), kind=kOutput, calls=%fused_computation.7 | convolution fusion | flops 11296309248 | bytes 32243712 | tf_op jit(solution)/shard_map/dot_general | solution.py:26
  36.9 0.0 all-reduce.11.cloned.1.call-update
  36.9 0.0 all-reduce.13.cloned.1.call-start
  37.0 39.1 %all-reduce.11.cloned.1.call-done = f32[2048,128]{1,0:T(8,128)} async-done(((f32[2048,128]{1,0:T(8,128)}), f32[2048,128]{1,0:T(8,128)}) %all-reduce.11.cloned.1.call-update) | async-done | bytes 1048592 | tf_op jit(solution)/shard_map/psum | solution.py:29
  76.1 0.0 all-reduce.13.cloned.1.call-update
  76.1 0.0 all-reduce.15.cloned.1.call-start
  76.2 54.7 %all-reduce.13.cloned.1.call-done = f32[2048,128]{1,0:T(8,128)} async-done(((f32[2048,128]{1,0:T(8,128)}), f32[2048,128]{1,0:T(8,128)}) %all-reduce.13.cloned.1.call-update) | async-done | bytes 1048592 | tf_op jit(solution)/shard_map/psum | solution.py:29
  130.9 4.0 fusion.19
  134.9 0.0 all-reduce.15.cloned.1.call-update
  134.9 0.2 all-reduce.17.cloned.1.call-start
  135.1 20.1 %all-reduce.15.cloned.1.call-done = f32[128,128]{0,1:T(8,128)} async-done(((f32[128,128]{0,1:T(8,128)}), f32[128,128]{0,1:T(8,128)}) %all-reduce.15.cloned.1.call-update) | async-done | bytes 65552 | tf_op jit(solution)/shard_map/psum | solution.py:31
  155.3 0.9 copy.6
  156.2 0.9 fusion.31
  157.1 11.7 %cholesky.44 = f32[128,128]{1,0:T(8,128)S(1)} custom-call(f32[128,128]{1,0:T(8,128)S(1)} %fusion.31), custom_call_target="Cholesky" | custom-call | tf_op jit(solution)/shard_map/jit(cholesky)/cholesky | solution.py:10
  168.8 0.6 compare_reduce_fusion.1
  169.4 0.7 fusion.26
  170.1 9.8 %custom-call.6 = f32[1,128,128]{1,2,0:T(8,128)S(1)} custom-call(f32[1,128,128]{2,1,0:T(8,128)S(1)} %fusion.26), custom_call_target="InvertDiagBlocksLowerTriangular" | custom-call | tf_op jit(solution)/shard_map/jit(_solve_triangular)/triangular_solve | solution.py:11
  179.9 2.3 fusion.13
  182.2 50.5 %fusion.4 = f32[3584,128]{1,0:T(8,128)} fusion(f32[128,2048]{1,0:T(8,128)S(1)} %fusion.13, bf16[1,2048,3584]{2,1,0:T(8,128)(2,1)} %param.7, bf16[1,2048,3584]{2,1,0:T(8,128)(2,1)} %param.6), kind=kOutput, calls=%fused_computation.5 | convolution fusion | flops 11296309248 | bytes 32243712 | tf_op jit(solution)/shard_map/dot_general | solution.py:33
  232.7 0.0 all-reduce.17.cloned.1.call-update
  232.7 0.0 all-reduce.19.cloned.1.call-start
  232.8 57.3 %all-reduce.17.cloned.1.call-done = f32[3584,128]{1,0:T(8,128)} async-done(((f32[3584,128]{1,0:T(8,128)}), f32[3584,128]{1,0:T(8,128)}) %all-reduce.17.cloned.1.call-update) | async-done | bytes 1835024 | tf_op jit(solution)/shard_map/psum | solution.py:40
  290.2 0.0 all-reduce.21.cloned.1.call-start
  290.2 79.8 %all-reduce.19.cloned.1.call-done = f32[3584,128]{1,0:T(8,128)} async-done(((f32[3584,128]{1,0:T(8,128)}), f32[3584,128]{1,0:T(8,128)}) %all-reduce.19.cloned.1.call-update) | async-done | bytes 1835024 | tf_op jit(solution)/shard_map/psum | solution.py:40
  370.0 28.3 %fusion.2 = f32[2048,128]{1,0:T(8,128)} fusion(bf16[1,2048,3584]{2,1,0:T(8,128)(2,1)} %param.7, bf16[1,2048,3584]{2,1,0:T(8,128)(2,1)} %param.6, f32[3584,128]{1,0:T(8,128)} %all-reduce.19.cloned.1.call-done), kind=kOutput, calls=%fused_computation.3 | convolution fusion | flops 11296768000 | bytes 32243712 | tf_op jit(solution)/shard_map/dot_general | solution.py:26
  398.3 0.0 all-reduce.21.cloned.1.call-update
  398.3 0.0 all-reduce.23.cloned.1.call-start
  398.4 35.4 %all-reduce.21.cloned.1.call-done = f32[2048,128]{1,0:T(8,128)} async-done(((f32[2048,128]{1,0:T(8,128)}), f32[2048,128]{1,0:T(8,128)}) %all-reduce.21.cloned.1.call-update) | async-done | bytes 1048592 | tf_op jit(solution)/shard_map/psum | solution.py:29
  433.8 0.0 all-reduce.25.cloned.1.call-start
  433.8 54.7 %all-reduce.23.cloned.1.call-done = f32[2048,128]{1,0:T(8,128)} async-done(((f32[2048,128]{1,0:T(8,128)}), f32[2048,128]{1,0:T(8,128)}) %all-reduce.23.cloned.1.call-update) | async-done | bytes 1048592 | tf_op jit(solution)/shard_map/psum | solution.py:29
  488.5 4.0 fusion.16
  492.5 0.5 all-reduce.27.cloned.1.call-start
  493.0 19.9 %all-reduce.25.cloned.1.call-done = f32[128,128]{0,1:T(8,128)} async-done(((f32[128,128]{0,1:T(8,128)}), f32[128,128]{0,1:T(8,128)}) %all-reduce.25.cloned.1.call-update) | async-done | bytes 65552 | tf_op jit(solution)/shard_map/psum | solution.py:31
  512.9 0.9 copy.8
  513.8 0.9 fusion.29
  514.7 11.7 %cholesky.55 = f32[128,128]{1,0:T(8,128)S(1)} custom-call(f32[128,128]{1,0:T(8,128)S(1)} %fusion.29), custom_call_target="Cholesky" | custom-call | tf_op jit(solution)/shard_map/jit(cholesky)/cholesky | solution.py:10
  526.4 0.6 compare_reduce_fusion
  527.1 0.7 fusion.27
  527.7 9.8 %custom-call.7 = f32[1,128,128]{1,2,0:T(8,128)S(1)} custom-call(f32[1,128,128]{2,1,0:T(8,128)S(1)} %fusion.27), custom_call_target="InvertDiagBlocksLowerTriangular" | custom-call | tf_op jit(solution)/shard_map/jit(_solve_triangular)/triangular_solve | solution.py:11
  537.6 2.3 fusion.11
  539.9 50.5 %fusion = f32[3584,128]{1,0:T(8,128)} fusion(f32[128,2048]{1,0:T(8,128)S(1)} %fusion.11, bf16[1,2048,3584]{2,1,0:T(8,128)(2,1)} %param.7, bf16[1,2048,3584]{2,1,0:T(8,128)(2,1)} %param.6), kind=kOutput, calls=%fused_computation.1 | convolution fusion | flops 11296309248 | bytes 32243712 | tf_op jit(solution)/shard_map/dot_general | solution.py:33
  590.3 0.0 all-reduce.29.cloned.1.call-start
  590.4 57.4 %all-reduce.27.cloned.1.call-done = f32[3584,128]{1,0:T(8,128)} async-done(((f32[3584,128]{1,0:T(8,128)}), f32[3584,128]{1,0:T(8,128)}) %all-reduce.27.cloned.1.call-update) | async-done | bytes 1835024 | tf_op jit(solution)/shard_map/psum | solution.py:40
  647.8 79.8 %all-reduce.29.cloned.1.call-done = f32[3584,128]{1,0:T(8,128)} async-done(((f32[3584,128]{1,0:T(8,128)}), f32[3584,128]{1,0:T(8,128)}) %all-reduce.29.cloned.1.call-update) | async-done | bytes 1835024 | tf_op jit(solution)/shard_map/psum | solution.py:40
  727.6 1.8 broadcast_multiply_fusion
  729.4 32.2 %fusion.9 = bf16[1,2048,3584]{2,1,0:T(8,128)(2,1)} fusion(f32[128,2048]{1,0:T(8,128)S(1)} %fusion.11, f32[3584,128]{1,0:T(8,128)S(1)} %broadcast_multiply_fusion, bf16[1,2048,3584]{2,1,0:T(8,128)(2,1)} %param.7, bf16[1,2048,3584]{2,1,0:T(8,128)(2,1)} %param.6), kind=kOutput, calls=%fused_computation.11 | convolution fusion | flops 11310989312 | bytes 46923776 | tf_op jit(solution)/shard_map/dot_general | solution.py:41
  (12 shorter events, 0.2 us)
Async XLA Ops:
  7.2 1.5 copy-start
  7.2 68.9 %all-reduce.11.cloned.1.call-start = ((), (), s32[]{:S(2)}) async-start(), calls=%async_computation | async-start | bytes 2097152 | tf_op jit(solution)/shard_map/psum | solution.py:29
  36.9 93.9 %all-reduce.13.cloned.1.call-start = ((), (), s32[]{:S(2)}) async-start(), calls=%async_computation.1 | async-start | bytes 2097152 | tf_op jit(solution)/shard_map/psum | solution.py:29
  76.1 79.1 %all-reduce.15.cloned.1.call-start = ((), (), s32[]{:S(2)}) async-start(), calls=%async_computation.2 | async-start | bytes 131072 | tf_op jit(solution)/shard_map/psum | solution.py:31
  134.9 155.2 %all-reduce.17.cloned.1.call-start = ((), (), s32[]{:S(2)}) async-start(), calls=%async_computation.3 | async-start | bytes 3670016 | tf_op jit(solution)/shard_map/psum | solution.py:40
  232.7 137.3 %all-reduce.19.cloned.1.call-start = ((), (), s32[]{:S(2)}) async-start(), calls=%async_computation.4 | async-start | bytes 3670016 | tf_op jit(solution)/shard_map/psum | solution.py:40
  290.2 143.6 %all-reduce.21.cloned.1.call-start = ((), (), s32[]{:S(2)}) async-start(), calls=%async_computation.5 | async-start | bytes 2097152 | tf_op jit(solution)/shard_map/psum | solution.py:29
  398.3 90.2 %all-reduce.23.cloned.1.call-start = ((), (), s32[]{:S(2)}) async-start(), calls=%async_computation.6 | async-start | bytes 2097152 | tf_op jit(solution)/shard_map/psum | solution.py:29
  433.8 79.1 %all-reduce.25.cloned.1.call-start = ((), (), s32[]{:S(2)}) async-start(), calls=%async_computation.7 | async-start | bytes 131072 | tf_op jit(solution)/shard_map/psum | solution.py:31
  492.5 155.2 %all-reduce.27.cloned.1.call-start = ((), (), s32[]{:S(2)}) async-start(), calls=%async_computation.8 | async-start | bytes 3670016 | tf_op jit(solution)/shard_map/psum | solution.py:40
  590.3 137.3 %all-reduce.29.cloned.1.call-start = ((), (), s32[]{:S(2)}) async-start(), calls=%async_computation.9 | async-start | bytes 3670016 | tf_op jit(solution)/shard_map/psum | solution.py:40
  727.6 34.0 %copy-start.1 = (f32[3584,128]{1,0:T(8,128)S(1)}, f32[3584,128]{1,0:T(8,128)}, u32[]{:S(2)}) copy-start(f32[3584,128]{1,0:T(8,128)} %param.8) | copy-start | bytes 5505028
  729.4 32.2 %copy-start.2 = (f32[3584,128]{1,0:T(8,128)}, f32[3584,128]{1,0:T(8,128)S(1)}, u32[]{:S(2)}) copy-start(f32[3584,128]{1,0:T(8,128)S(1)} %broadcast_multiply_fusion) | copy-start | bytes 5505028
Sparse Core Ops, SparseCore 0:
  37.1 39.0 all-reduce.10
  78.5 52.3 all-reduce.12
  135.0 20.1 all-reduce.14
  232.9 57.2 all-reduce.16
  292.3 77.6 all-reduce.18
  398.4 35.2 all-reduce.20
  436.1 52.3 all-reduce.22
  492.6 20.1 all-reduce.24
  590.5 57.2 all-reduce.26
  650.0 77.6 all-reduce.28
